TPU v7x, 32 devices: a whole 2x2x4 slice. The times are simulated.
32 devices in a mesh: row: 2 (over core), col: 16 (over z, y, x).
Axes of the slice: x: 2, y: 2, z: 4, core: 2. Of those that a mesh axis runs over, the one named last changes fastest.
Arguments:
- object_in: float32 [2, 2, 512, 4096], P(None, None, 'row', 'col'), may hold values from -4 to 4
- probe_in: float32 [2, 256, 256], replicated, may hold values from -5 to 5
- positions: int32 [2, 16, 2, 2], P('row', 'col'), may hold values from -32 to 32
- intensity: float32 [2, 16, 2, 256, 256], P('row', 'col'), may hold values from 0.1 to 8.2
Outputs:
- object_out: float32 [2, 2, 512, 4096], P(None, None, 'row', 'col')
- probe_out: float32 [2, 256, 256], replicated
Inputs may be any that keep to these rules, and one draw needn't show every extreme that they name: positions[r, c, p] = (dy, dx) places the probe of position p on object rows r * 256 + dy to r * 256 + dy + 255 and columns c * 256 + dx to c * 256 + dx + 255.
All inputs are finite; a program needn't handle non-finite values.
Results may differ from a plain program's by a relative error of at most 0.0003.
Values sent between devices are 32-bit elements; how exact they have to be, the bound alone decides.
No kernel may reach another device: no remote copies, remote signals or barrier semaphores. Data moves between devices by JAX's collectives and lax.ppermute only.
A program may use at most 64 MiB of HBM per device.

v0:
```python
import math
import jax
import jax.numpy as jnp
from jax import lax
from jax.sharding import PartitionSpec as P

RIM = 32


def passed_along(value, axis, steps):
    count = lax.axis_size(axis)
    initial, last = (max(0, -steps), min(count, count - steps))
    return lax.ppermute(value, axis, [(source, source + steps) for source in range(initial, last)])


def extended(cells, sides, width):
    for axis, dim in sides:
        count = lax.axis_size(axis)
        ends = count - 1
        head = lax.slice_in_dim(cells, 0, width, axis=dim)
        tail = lax.slice_in_dim(cells, cells.shape[dim] - width, cells.shape[dim], axis=dim)
        cells = jnp.concatenate(
            [
                lax.ppermute(tail, axis, [(i, (i + 1) % count) for i in range(ends)]),
                cells,
                lax.ppermute(head, axis, [((i + 1) % count, i) for i in range(ends)]),
            ],
            axis=dim,
        )
    return cells


def tables(extent):
    line_idx = jnp.arange(extent, dtype=jnp.int32)
    turn_count = line_idx[:, None] * line_idx[None, :] % extent
    angles = turn_count.astype(jnp.float32) * (2.0 * math.pi / extent)
    factor = 1.0 / math.sqrt(extent)
    cosine = jnp.cos(angles) * factor
    sine_tab = jnp.sin(angles) * factor
    frequency = ((line_idx + extent // 2) % extent - extent // 2).astype(jnp.float32)
    phases = (
        -math.pi * 8.0 / (extent * extent) * (frequency[:, None] ** 2 + frequency[None, :] ** 2)
    )
    return (cosine, sine_tab, jnp.cos(phases), jnp.sin(phases))


def matrices(cosine, sine_tab, orient):
    return (cosine, sine_tab, float(orient))


def transform(real_part, imag_part, tables_pair):
    cosine, sine_tab, orient = tables_pair
    high = lax.Precision.HIGHEST
    rc = jnp.einsum("byx,xk->byk", real_part, cosine, precision=high)
    rs = jnp.einsum("byx,xk->byk", real_part, sine_tab, precision=high)
    ic = jnp.einsum("byx,xk->byk", imag_part, cosine, precision=high)
    isn = jnp.einsum("byx,xk->byk", imag_part, sine_tab, precision=high)
    mid_re = rc + orient * isn
    mid_im = ic - orient * rs
    out_re = jnp.einsum("ky,byx->bkx", cosine, mid_re, precision=high) + orient * jnp.einsum(
        "ky,byx->bkx", sine_tab, mid_im, precision=high
    )
    out_im = jnp.einsum("ky,byx->bkx", cosine, mid_im, precision=high) - orient * jnp.einsum(
        "ky,byx->bkx", sine_tab, mid_re, precision=high
    )
    return (out_re, out_im)


def times_plain(first_re, first_im, second_re, second_im):
    return (
        first_re * second_re - first_im * second_im,
        first_re * second_im + first_im * second_re,
    )


def times_conj(first_re, first_im, second_re, second_im):
    return (
        first_re * second_re + first_im * second_im,
        first_re * second_im - first_im * second_re,
    )


def tile_gradient(window, probe, offsets, measured, constants):
    cosine, sine_tab, kern_re, kern_im = constants
    forward = matrices(cosine, sine_tab, 1)
    backward = matrices(cosine, sine_tab, -1)
    extent = probe.shape[-1]
    zero_idx = jnp.zeros((), jnp.int32)

    def cut_patch(offset):
        return lax.dynamic_slice(
            window, (zero_idx, zero_idx, offset[0] + RIM, offset[1] + RIM), (2, 2, extent, extent)
        )

    patches = jax.vmap(cut_patch)(offsets)
    first_re, first_im = (patches[:, 0, 0], patches[:, 0, 1])
    second_re, second_im = (patches[:, 1, 0], patches[:, 1, 1])
    probe_re, probe_im = (probe[0], probe[1])
    wave_re, wave_im = times_plain(probe_re, probe_im, first_re, first_im)
    spec_re, spec_im = transform(wave_re, wave_im, forward)
    spec_re, spec_im = times_plain(kern_re, kern_im, spec_re, spec_im)
    prop_re, prop_im = transform(spec_re, spec_im, backward)
    exit_re, exit_im = times_plain(prop_re, prop_im, second_re, second_im)
    far_re, far_im = transform(exit_re, exit_im, forward)
    excess = 2.0 * (far_re * far_re + far_im * far_im - measured)
    back_re, back_im = transform(excess * far_re, excess * far_im, backward)
    grad2_re, grad2_im = times_conj(prop_re, prop_im, back_re, back_im)
    lift_re, lift_im = times_conj(second_re, second_im, back_re, back_im)
    lift_re, lift_im = transform(lift_re, lift_im, forward)
    lift_re, lift_im = times_conj(kern_re, kern_im, lift_re, lift_im)
    enter_re, enter_im = transform(lift_re, lift_im, backward)
    grad1_re, grad1_im = times_conj(probe_re, probe_im, enter_re, enter_im)
    probe_re_g, probe_im_g = times_conj(first_re, first_im, enter_re, enter_im)
    probe_grad = jnp.stack([jnp.sum(probe_re_g, 0), jnp.sum(probe_im_g, 0)], 0)
    pieces = jnp.stack([jnp.stack([grad1_re, grad1_im], 1), jnp.stack([grad2_re, grad2_im], 1)], 1)
    gradient = jnp.zeros(window.shape, jnp.float32)
    for position in range(offsets.shape[0]):
        start_at = (zero_idx, zero_idx, offsets[position, 0] + RIM, offsets[position, 1] + RIM)
        current = lax.dynamic_slice(gradient, start_at, pieces.shape[1:])
        gradient = lax.dynamic_update_slice(gradient, current + pieces[position], start_at)
    return (gradient, probe_grad)


def turned(block):
    return jnp.swapaxes(block, 2, 3)


def rows_then_cols(gradient):
    inner_px = gradient.shape[-1] - 2 * RIM
    upper_end = RIM + inner_px
    from_below = passed_along(gradient[:, :, :RIM, :], "row", -1)
    from_above = passed_along(gradient[:, :, upper_end:, :], "row", 1)
    middle = gradient[:, :, RIM:upper_end, :]
    middle = middle.at[:, :, inner_px - RIM :, :].add(from_below)
    middle = middle.at[:, :, :RIM, :].add(from_above)
    from_right = turned(passed_along(turned(middle[..., :RIM]), "col", -1))
    from_left = turned(passed_along(turned(middle[..., upper_end:]), "col", 1))
    interior = middle[..., RIM:upper_end]
    interior = interior.at[..., inner_px - RIM :].add(from_right)
    interior = interior.at[..., :RIM].add(from_left)
    return interior


def local(object_in, probe_in, positions, intensity):
    extent = probe_in.shape[-1]
    constants = tables(extent)
    offsets = positions.reshape(-1, 2)
    measured = intensity.reshape(-1, extent, extent)
    tile_total = lax.axis_size("row") * lax.axis_size("col")
    probe_rate = 2.0 / tile_total
    current = object_in
    window = extended(current, (("row", 2), ("col", 3)), RIM)
    gradient, probe_grad = tile_gradient(window, probe_in, offsets, measured, constants)
    probe_total = lax.psum(probe_grad, ("row", "col"))
    probe_next = probe_in - probe_rate * probe_total
    descent = rows_then_cols(gradient)
    local_peak = jnp.max(descent[:, 0] ** 2 + descent[:, 1] ** 2)
    largest = lax.pmax(local_peak, ("row", "col"))
    current = current - 0.3 * descent / (jnp.sqrt(largest) + 1e-06)
    return (current, probe_next)


def solution(mesh):
    placed = (
        P(None, None, "row", "col"),
        P(),
        P("row", "col", None, None),
        P("row", "col", None, None, None),
    )
    return jax.shard_map(
        local,
        mesh=mesh,
        in_specs=placed,
        out_specs=(P(None, None, "row", "col"), P()),
        check_vma=False,
    )
```

profile of v0, /device:TPU:0, one launch (start us, length us, event | category | flops | bytes accessed | tf_op | source)
XLA Modules:
  0.0 372.2 jit_solution(18278796465916017940)
XLA Ops:
  10.1 2.4 collective-permute-start
  22.2 2.0 copy.98
  24.5 4.2 %collective-permute-start.2 = (f32[2,2,320,32]{2,3,1,0:T(8,128)S(1)}, f32[2,2,320,32]{2,3,1,0:T(8,128)S(1)}, u32[]{:S(2)}, u32[]{:S(2)}) collective-permute-start(f32[2,2,320,32]{2,3,1,0:T(8,128)S(1)} %get-tuple-element.84), channel_id=1, source_target_pairs={{0,1},{1,2},{2,3},{3,4},{4,5},{5,6},{6,7},{7,8},{8,9},{9,10},{10,1... | collective-permute-start | bytes 491528 | tf_op jit(solution)/shard_map/ppermute | solution.py:24
  30.1 3.7 collective-permute-done.2
  33.8 6.2 %collective-permute-done.3 = f32[2,2,320,32]{2,3,1,0:T(8,128)S(1)} collective-permute-done((f32[2,2,320,32]{2,3,1,0:T(8,128)S(1)}, f32[2,2,320,32]{2,3,1,0:T(8,128)S(1)}, u32[]{:S(2)}, u32[]{:S(2)}) %collective-permute-start.3) | collective-permute-done | bytes 163872 | tf_op jit(solution)/shard_map/ppermute | solution.py:26
  41.8 11.3 %while.5 = (s32[]{:T(128)}, f32[2,2,320,320]{2,3,1,0:T(8,128)S(1)}, s32[2,4]{1,0:T(2,128)S(1)}, f32[2,2,2,256,256]{3,4,0,2,1:T(8,128)}, s32[]{:T(128)}) while((s32[]{:T(128)}, f32[2,2,320,320]{2,3,1,0:T(8,128)S(1)}, s32[2,4]{1,0:T(2,128)S(1)}, f32[2,2,2,256,256]{3,4,0,2,1:T(8,128)}, s32[]{:T(128)}) %tuple.62), condition=%wide.while_cond.4, body=%wide.while_body.4.sunk | while | flops 2 | bytes 21496496 | solution.py:91
  53.1 3.4 fusion.112
  56.5 3.2 fusion.116
  59.8 1.9 convolution_subtract_fusion.5
  63.5 1.9 convolution_add_fusion.5
  67.2 2.3 fusion.22
  71.4 1.9 fusion.108
  73.3 1.9 fusion.104
  75.1 1.9 fusion.21
  78.8 2.1 fusion.20
  84.6 1.9 fusion.32
  90.1 2.0 convolution_add_fusion.3
  94.0 1.8 convolution_subtract_fusion.3
  95.9 1.8 fusion.94
  97.7 1.8 fusion.15
  99.6 1.8 fusion.14
  101.4 1.9 fusion.92
  103.3 2.3 fusion.88
  105.7 1.9 fusion.13
  107.6 1.9 fusion.12
  115.1 2.2 add_bitcast_fusion
  119.0 1.8 fusion.84
  120.9 1.9 convolution_subtract_fusion.1
  124.6 1.8 convolution_add_fusion.1
  126.4 2.1 fusion.82
  128.5 1.8 fusion.6
  130.4 1.8 fusion.7
  132.2 1.9 fusion.76
  134.1 1.9 fusion.72
  136.0 1.9 fusion.5
  137.9 2.3 fusion.4
  145.6 2.8 fusion.38
  150.1 13.4 %dynamic_update_slice.6 = f32[2,2,320,320]{2,3,1,0:T(8,128)S(1)} dynamic-update-slice(f32[2,2,320,320]{2,3,1,0:T(8,128)S(1)} %broadcast_in_dim.2, f32[2,2,256,256]{2,3,1,0:T(8,128)} %fusion.25, s32[]{:T(128)} %constant.162.clone.1, s32[]{:T(128)} %constant.162.clone.1, s32[]{:T(128)S(6)} %select_n.155, s32[]{:T(128)S(6)} %select_n.156) | dynamic-update-slice | bytes 2097156 | tf_op jit(solution)/shard_map/dynamic_update_slice | solution.py:120
  163.5 2.4 fusion.27
  165.9 14.0 %dynamic_update_slice.7 = f32[2,2,320,320]{2,3,1,0:T(8,128)S(1)} dynamic-update-slice(f32[2,2,320,320]{2,3,1,0:T(8,128)S(1)} %dynamic_update_slice.6, f32[2,2,256,256]{2,3,1,0:T(8,128)} %fusion.27, s32[]{:T(128)} %constant.162.clone.1, s32[]{:T(128)} %constant.162.clone.1, s32[]{:T(128)S(6)} %select_n.157, s32[]{:T(128)S(6)} %select_n.158) | dynamic-update-slice | bytes 2097156 | tf_op jit(solution)/shard_map/dynamic_update_slice | solution.py:120
  181.8 2.0 copy.129
  187.1 4.4 %collective-permute-start.5 = (f32[2,2,32,320]{3,2,1,0:T(8,128)}, f32[2,2,32,320]{3,2,1,0:T(8,128)}, u32[]{:S(2)}, u32[]{:S(2)}) collective-permute-start(f32[2,2,32,320]{3,2,1,0:T(8,128)} %copy.126), channel_id=1, source_target_pairs={{0,16},{1,17},{2,18},{3,19},{4,20},{5,21},{6,22},{7,23},{8,24},{9,... | collective-permute-start | bytes 491528 | tf_op jit(solution)/shard_map/ppermute | solution.py:13
  192.8 3.7 %scatter-add.14 = f32[2,2,256,320]{2,3,1,0:T(8,128)} dynamic-update-slice(f32[2,2,256,320]{2,3,1,0:T(8,128)} %slice.249, f32[2,2,32,320]{2,3,1,0:T(8,128)S(1)} %slice_add_fusion.1, s32[]{:T(128)} %constant.162.clone.1, s32[]{:T(128)} %constant.162.clone.1, s32[]{:T(128)} %constant.175.clone.1, s32[]{:T(128)} %constant.162.clone.1) | dynamic-update-slice | bytes 327684 | tf_op jit(solution)/shard_map/scatter-add | solution.py:134
  198.8 3.6 scatter-add.15
  206.8 4.7 %collective-permute-start.7 = (f32[2,2,32,256]{3,2,1,0:T(8,128)S(1)}, f32[2,2,32,256]{3,2,1,0:T(8,128)S(1)}, u32[]{:S(2)}, u32[]{:S(2)}) collective-permute-start(f32[2,2,32,256]{3,2,1,0:T(8,128)S(1)} %get-tuple-element.90), channel_id=1, source_target_pairs={{0,1},{1,2},{2,3},{3,4},{4,5},{5,6},{6,7},{7,8},{8,9},{9,10},{10,1... | collective-permute-start | bytes 393224 | tf_op jit(solution)/shard_map/ppermute | solution.py:13
  211.5 105.9 %all-reduce.2.cloned.1.call-done = f32[2,256,256]{1,2,0:T(8,128)} async-done(((f32[2,256,256]{1,2,0:T(8,128)}), f32[2,256,256]{1,2,0:T(8,128)}) %all-reduce.2.cloned.1.call-update) | async-done | bytes 524304 | tf_op jit(solution)/shard_map/psum | solution.py:154
  321.3 39.5 %pmax.7 = f32[]{:T(128)} all-reduce(f32[]{:T(128)} %fusion.29), channel_id=1, replica_groups=mesh['row'=2,'col'=16] {'row','col'}, use_global_device_ids=true, to_apply=%region_1.2 | all-reduce | flops 1 | bytes 8 | tf_op jit(solution)/shard_map/pmax | solution.py:158
  362.6 2.5 copy.130
  (113 shorter events, 72.5 us)
Async XLA Ops:
  7.2 6.7 %copy-start.15 = (s32[1,1,2,2]{3,2,1,0:T(2,128)S(1)}, s32[1,1,2,2]{3,2,1,0:T(2,128)}, u32[]{:S(2)}) copy-start(s32[1,1,2,2]{3,2,1,0:T(2,128)} %param.14) | copy-start | bytes 52
  7.2 12.2 %copy-start.12 = (f32[2,256,256]{2,1,0:T(8,128)S(1)}, f32[2,256,256]{2,1,0:T(8,128)}, u32[]{:S(2)}) copy-start(f32[2,256,256]{2,1,0:T(8,128)} %param.13) | copy-start | bytes 1572868
  7.2 310.2 %all-reduce.2.cloned.1.call-start = ((), (), s32[]{:S(2)}) async-start(), calls=%async_computation | async-start | bytes 1048576 | tf_op jit(solution)/shard_map/psum | solution.py:154
  8.8 31.1 %copy-start.2 = (f32[2,2,256,256]{2,3,1,0:T(8,128)}, f32[2,2,256,256]{2,3,1,0:T(8,128)S(1)}, u32[]{:S(2)}) copy-start(f32[2,2,256,256]{2,3,1,0:T(8,128)S(1)} %copy.128) | copy-start | bytes 3145732
  10.1 14.2 %collective-permute-start = (f32[2,2,32,256]{2,3,1,0:T(8,128)}, f32[2,2,32,256]{2,3,1,0:T(8,128)S(1)}, u32[]{:S(2)}, u32[]{:S(2)}) collective-permute-start(f32[2,2,32,256]{2,3,1,0:T(8,128)} %get-tuple-element.96), channel_id=1, source_target_pairs={{0,16},{1,17},{2,18},{3,19},{4,20},{5,21},{6,22},{7,23},{8,24},{9,... | collective-permute-start | bytes 393224 | tf_op jit(solution)/shard_map/ppermute | solution.py:24
  12.5 11.7 %collective-permute-start.1 = (f32[2,2,32,256]{2,3,1,0:T(8,128)}, f32[2,2,32,256]{2,3,1,0:T(8,128)S(1)}, u32[]{:S(2)}, u32[]{:S(2)}) collective-permute-start(f32[2,2,32,256]{2,3,1,0:T(8,128)} %get-tuple-element.97), channel_id=1, source_target_pairs={{16,0},{17,1},{18,2},{19,3},{20,4},{21,5},{22,6},{23,7},{24,8},{25... | collective-permute-start | bytes 393224 | tf_op jit(solution)/shard_map/ppermute | solution.py:26
  24.3 9.5 %copy-start.9 = (f32[2,2,32,256]{2,3,1,0:T(8,128)}, f32[2,2,32,256]{2,3,1,0:T(8,128)S(1)}, u32[]{:S(2)}) copy-start(f32[2,2,32,256]{2,3,1,0:T(8,128)S(1)} %collective-permute-done) | copy-start | bytes 393220
  24.3 9.5 %copy-start.10 = (f32[2,2,32,256]{2,3,1,0:T(8,128)}, f32[2,2,32,256]{2,3,1,0:T(8,128)S(1)}, u32[]{:S(2)}) copy-start(f32[2,2,32,256]{2,3,1,0:T(8,128)S(1)} %collective-permute-done.1) | copy-start | bytes 393220
  24.5 9.3 %collective-permute-start.2 = (f32[2,2,320,32]{2,3,1,0:T(8,128)S(1)}, f32[2,2,320,32]{2,3,1,0:T(8,128)S(1)}, u32[]{:S(2)}, u32[]{:S(2)}) collective-permute-start(f32[2,2,320,32]{2,3,1,0:T(8,128)S(1)} %get-tuple-element.84), channel_id=1, source_target_pairs={{0,1},{1,2},{2,3},{3,4},{4,5},{5,6},{6,7},{7,8},{8,9},{9,10},{10,1... | collective-permute-start | bytes 491528 | tf_op jit(solution)/shard_map/ppermute | solution.py:24
  28.7 11.2 %collective-permute-start.3 = (f32[2,2,320,32]{2,3,1,0:T(8,128)S(1)}, f32[2,2,320,32]{2,3,1,0:T(8,128)S(1)}, u32[]{:S(2)}, u32[]{:S(2)}) collective-permute-start(f32[2,2,320,32]{2,3,1,0:T(8,128)S(1)} %get-tuple-element.85), channel_id=1, source_target_pairs={{1,0},{2,1},{3,2},{4,3},{5,4},{6,5},{7,6},{8,7},{9,8},{10,9},{11,1... | collective-permute-start | bytes 491528 | tf_op jit(solution)/shard_map/ppermute | solution.py:26
  41.8 1.3 copy-start
  45.4 1.9 copy-start.1
  47.3 1.3 copy-start
  50.9 1.9 copy-start.1
  53.1 6.6 %copy-start.6 = (f32[256,256]{0,1:T(8,128)S(1)}, f32[256,256]{0,1:T(8,128)}, u32[]{:S(2)}) copy-start(f32[256,256]{0,1:T(8,128)} %copy.64) | copy-start | bytes 786436
  53.1 6.6 %copy-start.7 = (f32[256,256]{0,1:T(8,128)S(1)}, f32[256,256]{0,1:T(8,128)}, u32[]{:S(2)}) copy-start(f32[256,256]{0,1:T(8,128)} %copy.71) | copy-start | bytes 786436
  53.1 6.6 %copy-start.8 = (f32[2,2,2,256,256]{3,4,0,2,1:T(8,128)S(1)}, f32[2,2,2,256,256]{3,4,0,2,1:T(8,128)}, u32[]{:S(2)}) copy-start(f32[2,2,2,256,256]{3,4,0,2,1:T(8,128)} %get-tuple-element.57) | copy-start | bytes 6291460
  95.9 5.5 %copy-start.4 = (f32[1,1,2,256,256]{3,4,2,1,0:T(8,128)S(1)}, f32[1,1,2,256,256]{3,4,2,1,0:T(8,128)}, u32[]{:S(2)}) copy-start(f32[1,1,2,256,256]{3,4,2,1,0:T(8,128)} %copy.98) | copy-start | bytes 1572868
  148.6 1.3 copy-start.5
  180.4 5.0 %copy-start.13 = (f32[256,256]{0,1:T(8,128)S(1)}, f32[256,256]{0,1:T(8,128)}, u32[]{:S(2)}) copy-start(f32[256,256]{0,1:T(8,128)} %get-tuple-element.66) | copy-start | bytes 786436
  180.4 5.0 %copy-start.14 = (f32[256,256]{0,1:T(8,128)S(1)}, f32[256,256]{0,1:T(8,128)}, u32[]{:S(2)}) copy-start(f32[256,256]{0,1:T(8,128)} %get-tuple-element.67) | copy-start | bytes 786436
  180.4 11.1 %collective-permute-start.4 = (f32[2,2,32,320]{3,2,1,0:T(8,128)S(1)}, f32[2,2,32,320]{3,2,1,0:T(8,128)}, u32[]{:S(2)}, u32[]{:S(2)}) collective-permute-start(f32[2,2,32,320]{3,2,1,0:T(8,128)S(1)} %copy.124), channel_id=1, source_target_pairs={{16,0},{17,1},{18,2},{19,3},{20,4},{21,5},{22,6},{23,7},{24,8},{25... | collective-permute-start | bytes 491528 | tf_op jit(solution)/shard_map/ppermute | solution.py:13
  187.1 9.4 %collective-permute-start.5 = (f32[2,2,32,320]{3,2,1,0:T(8,128)}, f32[2,2,32,320]{3,2,1,0:T(8,128)}, u32[]{:S(2)}, u32[]{:S(2)}) collective-permute-start(f32[2,2,32,320]{3,2,1,0:T(8,128)} %copy.126), channel_id=1, source_target_pairs={{0,16},{1,17},{2,18},{3,19},{4,20},{5,21},{6,22},{7,23},{8,24},{9,... | collective-permute-start | bytes 491528 | tf_op jit(solution)/shard_map/ppermute | solution.py:13
  198.8 118.5 %copy-start.11 = (f32[2,256,256]{1,2,0:T(8,128)S(1)}, f32[2,256,256]{1,2,0:T(8,128)}, u32[]{:S(2)}) copy-start(f32[2,256,256]{1,2,0:T(8,128)} %copy.129) | copy-start | bytes 1572868
  205.5 113.0 %collective-permute-start.6 = (f32[2,2,32,256]{3,2,1,0:T(8,128)}, f32[2,2,32,256]{3,2,1,0:T(8,128)S(1)}, u32[]{:S(2)}, u32[]{:S(2)}) collective-permute-start(f32[2,2,32,256]{3,2,1,0:T(8,128)} %get-tuple-element.91), channel_id=1, source_target_pairs={{1,0},{2,1},{3,2},{4,3},{5,4},{6,5},{7,6},{8,7},{9,8},{10,9},{11,1... | collective-permute-start | bytes 393224 | tf_op jit(solution)/shard_map/ppermute | solution.py:13
  206.8 154.7 %copy-start.3 = (f32[2,2,256,256]{2,3,1,0:T(8,128)S(1)}, f32[2,2,256,256]{2,3,1,0:T(8,128)}, u32[]{:S(2)}) copy-start(f32[2,2,256,256]{2,3,1,0:T(8,128)} %copy-done.2) | copy-start | bytes 3145732
  206.8 112.6 %collective-permute-start.7 = (f32[2,2,32,256]{3,2,1,0:T(8,128)S(1)}, f32[2,2,32,256]{3,2,1,0:T(8,128)S(1)}, u32[]{:S(2)}, u32[]{:S(2)}) collective-permute-start(f32[2,2,32,256]{3,2,1,0:T(8,128)S(1)} %get-tuple-element.90), channel_id=1, source_target_pairs={{0,1},{1,2},{2,3},{3,4},{4,5},{5,6},{6,7},{7,8},{8,9},{9,10},{10,1... | collective-permute-start | bytes 393224 | tf_op jit(solution)/shard_map/ppermute | solution.py:13
Sparse Core Ops, SparseCore 0:
  186.3 130.9 all-reduce.1
where the time goes:
time: 377 us; the launch traced here: 372 us
  waiting for transfers between devices  116 us (31%)
  matrix products  94.9 us (25%)
  local copies, waits for them, and re-layouts  67.2 us (18%)
  blocking collectives  39.5 us (10%)
  starting transfers between devices  21 us (6%)
  between operations  20.6 us (5%)
  other arithmetic  12.9 us (3%)
    psum x1, waiting for transfers between devices, local(): probe_total = lax.psum(probe_grad, ('row', 'col'))  106 us
    pmax x1, blocking collectives, local(): largest = lax.pmax(local_peak, ('row', 'col'))  39.5 us
    dynamic_update_slice x2, local copies, waits for them, and re-layouts, tile_gradient(): lax.dynamic_update_slice(gradient, current + pieces[position], start_at)  27.5 us
    dot_general x6, matrix products, transform(): ic = jnp.einsum('byx,xk->byk', imag_part, cosine, precision=high)  13.1 us
    dot_general x6, matrix products, transform(): rc = jnp.einsum('byx,xk->byk', real_part, cosine, precision=high)  12.6 us
    dot_general x6, matrix products, transform(): jnp.einsum('ky,byx->bkx', sine_tab, mid_im, precision=high)  12.4 us
    dot_general x6, matrix products, transform(): rs = jnp.einsum('byx,xk->byk', real_part, sine_tab, precision=high)  11.8 us
    ppermute x4, starting transfers between devices, passed_along(): lax.ppermute(value, axis, [(source, source + steps) for source in range(i...  11.8 us
  transfers between devices with their start and end apart: 9, of which 3 were waited for; matrix products, arithmetic and copies ran while one was open for 7% of the time, Pallas kernels for 0%

commit v1 on v0

--- a/solution.py
+++ b/solution.py
@@ -151,7 +151,7 @@
     current = object_in
     window = extended(current, (("row", 2), ("col", 3)), RIM)
     gradient, probe_grad = tile_gradient(window, probe_in, offsets, measured, constants)
-    probe_total = lax.psum(probe_grad, ("row", "col"))
+    probe_total = jax.lax.psum(jax.lax.psum(probe_grad, "col"), "row")
     probe_next = probe_in - probe_rate * probe_total
     descent = rows_then_cols(gradient)
     local_peak = jnp.max(descent[:, 0] ** 2 + descent[:, 1] ** 2)

time: 377 us -> 356 us (0.944)
  waiting for transfers between devices: 116 us -> 97 us
    psum x1 -> x2, waiting for transfers between devices: 106 us -> 86.3 us  [local(): probe_total = jax.lax.psum(jax.lax.psum(probe_grad, 'col'), 'row')]
    unnamed x33 -> x29, local copies, waits for them, and re-layouts: 9.49 us -> 8.22 us
  transfers between devices with their start and end apart: 9 -> 10, of which waited for: 3 -> 4; matrix products, arithmetic and copies ran while one was open for 7% -> 8% of each run, Pallas kernels for 0% -> 0%
where the time goes in v1:
time: 356 us; the launch traced here: 351 us
  waiting for transfers between devices  97 us (27%)
  matrix products  94.8 us (27%)
  local copies, waits for them, and re-layouts  65.3 us (18%)
  blocking collectives  39.5 us (11%)
  starting transfers between devices  20.9 us (6%)
  between operations  20.6 us (6%)
  other arithmetic  12.8 us (4%)
    psum x2, waiting for transfers between devices, local(): probe_total = jax.lax.psum(jax.lax.psum(probe_grad, 'col'), 'row')  86.3 us
    pmax x1, blocking collectives, local(): largest = lax.pmax(local_peak, ('row', 'col'))  39.5 us
    dynamic_update_slice x2, local copies, waits for them, and re-layouts, tile_gradient(): lax.dynamic_update_slice(gradient, current + pieces[position], start_at)  27.5 us
    dot_general x6, matrix products, transform(): ic = jnp.einsum('byx,xk->byk', imag_part, cosine, precision=high)  13.1 us
    dot_general x6, matrix products, transform(): rc = jnp.einsum('byx,xk->byk', real_part, cosine, precision=high)  12.6 us
    dot_general x6, matrix products, transform(): jnp.einsum('ky,byx->bkx', sine_tab, mid_im, precision=high)  12.2 us
    dot_general x6, matrix products, transform(): rs = jnp.einsum('byx,xk->byk', real_part, sine_tab, precision=high)  11.8 us
    ppermute x4, starting transfers between devices, passed_along(): lax.ppermute(value, axis, [(source, source + steps) for source in range(i...  11.6 us
  transfers between devices with their start and end apart: 10, of which 4 were waited for; matrix products, arithmetic and copies ran while one was open for 8% of the time, Pallas kernels for 0%

profile of v1, /device:TPU:0, one launch (start us, length us, event | category | flops | bytes accessed | tf_op | source)
XLA Modules:
  0.0 351.2 jit_solution(4191340781180632826)
XLA Ops:
  10.1 2.4 collective-permute-start
  22.3 2.0 copy.98
  24.6 4.2 %collective-permute-start.2 = (f32[2,2,320,32]{2,3,1,0:T(8,128)S(1)}, f32[2,2,320,32]{2,3,1,0:T(8,128)S(1)}, u32[]{:S(2)}, u32[]{:S(2)}) collective-permute-start(f32[2,2,320,32]{2,3,1,0:T(8,128)S(1)} %get-tuple-element.84), channel_id=1, source_target_pairs={{0,1},{1,2},{2,3},{3,4},{4,5},{5,6},{6,7},{7,8},{8,9},{9,10},{10,1... | collective-permute-start | bytes 491528 | tf_op jit(solution)/shard_map/ppermute | solution.py:24
  30.2 3.7 %collective-permute-done.2 = f32[2,2,320,32]{2,3,1,0:T(8,128)S(1)} collective-permute-done((f32[2,2,320,32]{2,3,1,0:T(8,128)S(1)}, f32[2,2,320,32]{2,3,1,0:T(8,128)S(1)}, u32[]{:S(2)}, u32[]{:S(2)}) %collective-permute-start.2) | collective-permute-done | bytes 163872 | tf_op jit(solution)/shard_map/ppermute | solution.py:24
  33.9 6.2 %collective-permute-done.3 = f32[2,2,320,32]{2,3,1,0:T(8,128)S(1)} collective-permute-done((f32[2,2,320,32]{2,3,1,0:T(8,128)S(1)}, f32[2,2,320,32]{2,3,1,0:T(8,128)S(1)}, u32[]{:S(2)}, u32[]{:S(2)}) %collective-permute-start.3) | collective-permute-done | bytes 163872 | tf_op jit(solution)/shard_map/ppermute | solution.py:26
  41.9 11.4 %while.5 = (s32[]{:T(128)}, f32[2,2,320,320]{2,3,1,0:T(8,128)S(1)}, s32[2,4]{1,0:T(2,128)S(1)}, f32[2,2,2,256,256]{3,4,0,2,1:T(8,128)}, s32[]{:T(128)}) while((s32[]{:T(128)}, f32[2,2,320,320]{2,3,1,0:T(8,128)S(1)}, s32[2,4]{1,0:T(2,128)S(1)}, f32[2,2,2,256,256]{3,4,0,2,1:T(8,128)}, s32[]{:T(128)}) %tuple.62), condition=%wide.while_cond.4, body=%wide.while_body.4.sunk | while | flops 2 | bytes 21496496 | solution.py:91
  53.4 3.4 fusion.112
  56.7 3.2 fusion.116
  60.0 1.9 convolution_subtract_fusion.5
  63.7 1.9 convolution_add_fusion.5
  67.4 2.3 fusion.22
  71.6 1.9 fusion.108
  73.5 1.9 fusion.104
  75.4 1.9 fusion.21
  79.1 2.1 fusion.20
  84.8 1.9 fusion.32
  88.5 1.8 fusion.96
  90.3 2.1 convolution_add_fusion.3
  101.6 1.9 fusion.92
  103.5 2.3 fusion.88
  105.8 1.9 fusion.13
  107.8 1.9 fusion.12
  113.4 1.8 fusion.9
  115.2 2.1 add_bitcast_fusion
  117.4 1.8 fusion.80
  119.2 1.8 fusion.84
  121.1 1.9 convolution_subtract_fusion.1
  124.8 1.9 convolution_add_fusion.1
  126.6 2.1 fusion.82
  128.7 1.8 fusion.6
  130.5 1.8 fusion.7
  132.4 1.9 fusion.76
  134.3 1.9 fusion.72
  136.2 1.9 fusion.5
  138.1 2.3 fusion.4
  145.8 2.7 fusion.38
  150.2 13.5 %dynamic_update_slice.6 = f32[2,2,320,320]{2,3,1,0:T(8,128)S(1)} dynamic-update-slice(f32[2,2,320,320]{2,3,1,0:T(8,128)S(1)} %broadcast_in_dim.2, f32[2,2,256,256]{2,3,1,0:T(8,128)} %fusion.25, s32[]{:T(128)} %constant.162.clone.1, s32[]{:T(128)} %constant.162.clone.1, s32[]{:T(128)S(6)} %select_n.155, s32[]{:T(128)S(6)} %select_n.156) | dynamic-update-slice | bytes 2097156 | tf_op jit(solution)/shard_map/dynamic_update_slice | solution.py:120
  163.6 2.4 fusion.27
  166.0 14.0 %dynamic_update_slice.7 = f32[2,2,320,320]{2,3,1,0:T(8,128)S(1)} dynamic-update-slice(f32[2,2,320,320]{2,3,1,0:T(8,128)S(1)} %dynamic_update_slice.6, f32[2,2,256,256]{2,3,1,0:T(8,128)} %fusion.27, s32[]{:T(128)} %constant.162.clone.1, s32[]{:T(128)} %constant.162.clone.1, s32[]{:T(128)S(6)} %select_n.157, s32[]{:T(128)S(6)} %select_n.158) | dynamic-update-slice | bytes 2097156 | tf_op jit(solution)/shard_map/dynamic_update_slice | solution.py:120
  186.9 4.4 %collective-permute-start.5 = (f32[2,2,32,320]{3,2,1,0:T(8,128)S(1)}, f32[2,2,32,320]{3,2,1,0:T(8,128)}, u32[]{:S(2)}, u32[]{:S(2)}) collective-permute-start(f32[2,2,32,320]{3,2,1,0:T(8,128)S(1)} %copy.126), channel_id=1, source_target_pairs={{0,16},{1,17},{2,18},{3,19},{4,20},{5,21},{6,22},{7,23},{8,24},{9,... | collective-permute-start | bytes 491528 | tf_op jit(solution)/shard_map/ppermute | solution.py:13
  191.3 2.0 copy.125
  193.3 2.0 slice_add_fusion.1
  195.3 4.3 %scatter-add.14 = f32[2,2,256,320]{2,3,1,0:T(8,128)S(1)} dynamic-update-slice(f32[2,2,256,320]{2,3,1,0:T(8,128)S(1)} %slice.249, f32[2,2,32,320]{2,3,1,0:T(8,128)} %slice_add_fusion.1, s32[]{:T(128)} %constant.162.clone.1, s32[]{:T(128)} %constant.162.clone.1, s32[]{:T(128)} %constant.175.clone.1, s32[]{:T(128)} %constant.162.clone.1) | dynamic-update-slice | bytes 327684 | tf_op jit(solution)/shard_map/scatter-add | solution.py:134
  200.9 2.7 scatter-add.15
  205.7 4.7 %collective-permute-start.7 = (f32[2,2,32,256]{3,2,1,0:T(8,128)}, f32[2,2,32,256]{3,2,1,0:T(8,128)S(1)}, u32[]{:S(2)}, u32[]{:S(2)}) collective-permute-start(f32[2,2,32,256]{3,2,1,0:T(8,128)} %get-tuple-element.90), channel_id=1, source_target_pairs={{0,1},{1,2},{2,3},{3,4},{4,5},{5,6},{6,7},{7,8},{8,9},{9,10},{10,1... | collective-permute-start | bytes 393224 | tf_op jit(solution)/shard_map/ppermute | solution.py:13
  211.2 86.3 %all-reduce.3.cloned.1.call-done = f32[2,256,256]{1,2,0:T(8,128)} async-done(((f32[2,256,256]{1,2,0:T(8,128)}), f32[2,256,256]{1,2,0:T(8,128)}) %all-reduce.3.cloned.1.call-update) | async-done | bytes 524304 | tf_op jit(solution)/shard_map/psum | solution.py:154
  298.4 2.0 copy.129
  300.4 39.5 %pmax.7 = f32[]{:T(128)} all-reduce(f32[]{:T(128)} %fusion.29), channel_id=1, replica_groups=mesh['row'=2,'col'=16] {'row','col'}, use_global_device_ids=true, to_apply=%region_1.2 | all-reduce | flops 1 | bytes 8 | tf_op jit(solution)/shard_map/pmax | solution.py:158
  (112 shorter events, 71.8 us)
Async XLA Ops:
  7.2 6.7 %copy-start.13 = (s32[1,1,2,2]{3,2,1,0:T(2,128)S(1)}, s32[1,1,2,2]{3,2,1,0:T(2,128)}, u32[]{:S(2)}) copy-start(s32[1,1,2,2]{3,2,1,0:T(2,128)} %param.14) | copy-start | bytes 52
  7.2 12.3 %copy-start.12 = (f32[2,256,256]{2,1,0:T(8,128)S(1)}, f32[2,256,256]{2,1,0:T(8,128)}, u32[]{:S(2)}) copy-start(f32[2,256,256]{2,1,0:T(8,128)} %param.13) | copy-start | bytes 1572868
  7.2 290.3 %all-reduce.3.cloned.1.call-start = ((), (), s32[]{:S(2)}) async-start(), calls=%async_computation | async-start | bytes 1048576 | tf_op jit(solution)/shard_map/psum | solution.py:154
  8.8 31.2 %copy-start.2 = (f32[2,2,256,256]{2,3,1,0:T(8,128)}, f32[2,2,256,256]{2,3,1,0:T(8,128)S(1)}, u32[]{:S(2)}) copy-start(f32[2,2,256,256]{2,3,1,0:T(8,128)S(1)} %copy.128) | copy-start | bytes 3145732
  10.1 14.3 %collective-permute-start = (f32[2,2,32,256]{2,3,1,0:T(8,128)}, f32[2,2,32,256]{2,3,1,0:T(8,128)S(1)}, u32[]{:S(2)}, u32[]{:S(2)}) collective-permute-start(f32[2,2,32,256]{2,3,1,0:T(8,128)} %get-tuple-element.96), channel_id=1, source_target_pairs={{0,16},{1,17},{2,18},{3,19},{4,20},{5,21},{6,22},{7,23},{8,24},{9,... | collective-permute-start | bytes 393224 | tf_op jit(solution)/shard_map/ppermute | solution.py:24
  12.5 11.9 %collective-permute-start.1 = (f32[2,2,32,256]{2,3,1,0:T(8,128)}, f32[2,2,32,256]{2,3,1,0:T(8,128)S(1)}, u32[]{:S(2)}, u32[]{:S(2)}) collective-permute-start(f32[2,2,32,256]{2,3,1,0:T(8,128)} %get-tuple-element.97), channel_id=1, source_target_pairs={{16,0},{17,1},{18,2},{19,3},{20,4},{21,5},{22,6},{23,7},{24,8},{25... | collective-permute-start | bytes 393224 | tf_op jit(solution)/shard_map/ppermute | solution.py:26
  24.4 9.5 %copy-start.9 = (f32[2,2,32,256]{2,3,1,0:T(8,128)}, f32[2,2,32,256]{2,3,1,0:T(8,128)S(1)}, u32[]{:S(2)}) copy-start(f32[2,2,32,256]{2,3,1,0:T(8,128)S(1)} %collective-permute-done) | copy-start | bytes 393220
  24.4 9.5 %copy-start.10 = (f32[2,2,32,256]{2,3,1,0:T(8,128)}, f32[2,2,32,256]{2,3,1,0:T(8,128)S(1)}, u32[]{:S(2)}) copy-start(f32[2,2,32,256]{2,3,1,0:T(8,128)S(1)} %collective-permute-done.1) | copy-start | bytes 393220
  24.6 9.3 %collective-permute-start.2 = (f32[2,2,320,32]{2,3,1,0:T(8,128)S(1)}, f32[2,2,320,32]{2,3,1,0:T(8,128)S(1)}, u32[]{:S(2)}, u32[]{:S(2)}) collective-permute-start(f32[2,2,320,32]{2,3,1,0:T(8,128)S(1)} %get-tuple-element.84), channel_id=1, source_target_pairs={{0,1},{1,2},{2,3},{3,4},{4,5},{5,6},{6,7},{7,8},{8,9},{9,10},{10,1... | collective-permute-start | bytes 491528 | tf_op jit(solution)/shard_map/ppermute | solution.py:24
  28.8 11.2 %collective-permute-start.3 = (f32[2,2,320,32]{2,3,1,0:T(8,128)S(1)}, f32[2,2,320,32]{2,3,1,0:T(8,128)S(1)}, u32[]{:S(2)}, u32[]{:S(2)}) collective-permute-start(f32[2,2,320,32]{2,3,1,0:T(8,128)S(1)} %get-tuple-element.85), channel_id=1, source_target_pairs={{1,0},{2,1},{3,2},{4,3},{5,4},{6,5},{7,6},{8,7},{9,8},{10,9},{11,1... | collective-permute-start | bytes 491528 | tf_op jit(solution)/shard_map/ppermute | solution.py:26
  41.9 1.3 copy-start
  45.6 1.9 copy-start.1
  47.5 1.3 copy-start
  51.1 1.9 copy-start.1
  53.3 6.6 %copy-start.6 = (f32[256,256]{0,1:T(8,128)S(1)}, f32[256,256]{0,1:T(8,128)}, u32[]{:S(2)}) copy-start(f32[256,256]{0,1:T(8,128)} %copy.64) | copy-start | bytes 786436
  53.3 6.6 %copy-start.7 = (f32[256,256]{0,1:T(8,128)S(1)}, f32[256,256]{0,1:T(8,128)}, u32[]{:S(2)}) copy-start(f32[256,256]{0,1:T(8,128)} %copy.71) | copy-start | bytes 786436
  53.3 6.6 %copy-start.8 = (f32[2,2,2,256,256]{3,4,0,2,1:T(8,128)S(1)}, f32[2,2,2,256,256]{3,4,0,2,1:T(8,128)}, u32[]{:S(2)}) copy-start(f32[2,2,2,256,256]{3,4,0,2,1:T(8,128)} %get-tuple-element.57) | copy-start | bytes 6291460
  96.1 5.5 %copy-start.4 = (f32[1,1,2,256,256]{3,4,2,1,0:T(8,128)S(1)}, f32[1,1,2,256,256]{3,4,2,1,0:T(8,128)}, u32[]{:S(2)}) copy-start(f32[1,1,2,256,256]{3,4,2,1,0:T(8,128)} %copy.98) | copy-start | bytes 1572868
  148.7 1.3 copy-start.5
  182.0 9.2 %collective-permute-start.4 = (f32[2,2,32,320]{3,2,1,0:T(8,128)}, f32[2,2,32,320]{3,2,1,0:T(8,128)}, u32[]{:S(2)}, u32[]{:S(2)}) collective-permute-start(f32[2,2,32,320]{3,2,1,0:T(8,128)} %copy.124), channel_id=1, source_target_pairs={{16,0},{17,1},{18,2},{19,3},{20,4},{21,5},{22,6},{23,7},{24,8},{25... | collective-permute-start | bytes 491528 | tf_op jit(solution)/shard_map/ppermute | solution.py:13
  185.5 156.5 %all-reduce.5.cloned.1.call-start = ((), (), s32[]{:S(2)}) async-start(), calls=%async_computation.1 | async-start | bytes 1048576 | tf_op jit(solution)/shard_map/psum | solution.py:154
  186.9 12.8 %collective-permute-start.5 = (f32[2,2,32,320]{3,2,1,0:T(8,128)S(1)}, f32[2,2,32,320]{3,2,1,0:T(8,128)}, u32[]{:S(2)}, u32[]{:S(2)}) collective-permute-start(f32[2,2,32,320]{3,2,1,0:T(8,128)S(1)} %copy.126), channel_id=1, source_target_pairs={{0,16},{1,17},{2,18},{3,19},{4,20},{5,21},{6,22},{7,23},{8,24},{9,... | collective-permute-start | bytes 491528 | tf_op jit(solution)/shard_map/ppermute | solution.py:13
  204.3 6.8 %collective-permute-start.6 = (f32[2,2,32,256]{3,2,1,0:T(8,128)S(1)}, f32[2,2,32,256]{3,2,1,0:T(8,128)S(1)}, u32[]{:S(2)}, u32[]{:S(2)}) collective-permute-start(f32[2,2,32,256]{3,2,1,0:T(8,128)S(1)} %get-tuple-element.91), channel_id=1, source_target_pairs={{1,0},{2,1},{3,2},{4,3},{5,4},{6,5},{7,6},{8,7},{9,8},{10,9},{11,1... | collective-permute-start | bytes 393224 | tf_op jit(solution)/shard_map/ppermute | solution.py:13
  205.7 134.9 %copy-start.3 = (f32[2,2,256,256]{2,3,1,0:T(8,128)S(1)}, f32[2,2,256,256]{2,3,1,0:T(8,128)}, u32[]{:S(2)}) copy-start(f32[2,2,256,256]{2,3,1,0:T(8,128)} %copy-done.2) | copy-start | bytes 3145732
  205.7 91.8 %collective-permute-start.7 = (f32[2,2,32,256]{3,2,1,0:T(8,128)}, f32[2,2,32,256]{3,2,1,0:T(8,128)S(1)}, u32[]{:S(2)}, u32[]{:S(2)}) collective-permute-start(f32[2,2,32,256]{3,2,1,0:T(8,128)} %get-tuple-element.90), channel_id=1, source_target_pairs={{0,1},{1,2},{2,3},{3,4},{4,5},{5,6},{6,7},{7,8},{8,9},{9,10},{10,1... | collective-permute-start | bytes 393224 | tf_op jit(solution)/shard_map/ppermute | solution.py:13
  340.7 1.3 copy-start.11
Sparse Core Ops, SparseCore 0:
  185.7 111.8 all-reduce.2
  299.9 17.5 all-reduce.4
